TPU v7x, 256 devices: a whole 4x4x8 slice. The times are simulated.
256 devices in a mesh: freq: 16 (over y, x), param: 4 (over z_hi, core), sens: 4 (over z_lo).
Axes of the slice: x: 4, y: 4, z: 8 (z_hi: 2, z_lo: 4; z = z_hi * 4 + z_lo), core: 2. Of those that a mesh axis runs over, the one named last changes fastest.
Arguments:
- series: bfloat16 [8, 600, 416], P(None, 'sens', 'freq'), may hold values from -6 to 6
- kernel: bfloat16 [2, 256, 600, 4096], P(None, 'freq', 'sens', 'param'), may hold values from -0.1875 to 0.1875
- prior_spectrum: float32 [256], P('freq'), may hold values from 0.3 to 1.5
- prior_scale: float32 [4096], P('param'), may hold values from 0.5 to 2
Outputs:
- adjoint_map: float32 [416, 8, 4096], P('freq', 'sens', 'param')
All inputs are finite; a program needn't handle non-finite values.
Results may differ from a plain program's by a relative error of at most 0.0047.
Values may be sent and summed in bfloat16 or wider, within the bound.
A program may use at most 64 MiB of HBM per device.

v0:
```python
import math

import jax
import jax.numpy as jnp
from jax import lax
from jax.sharding import PartitionSpec as P

LEN = 840
FB_DEV = 16


def joined_along(blocks, dim):
    blocks = jnp.moveaxis(blocks, 0, dim)
    lengths = blocks.shape
    return blocks.reshape(*lengths[:dim], lengths[dim] * lengths[dim + 1], *lengths[dim + 2 :])


def copy_for_each(x, axis):
    copies = jnp.broadcast_to(x, (lax.axis_size(axis), *x.shape))
    return lax.all_to_all(copies, axis, split_axis=0, concat_axis=0, tiled=True)


def gather_directly(x, axis, dim):
    return joined_along(copy_for_each(x, axis), dim)


def in_blocks(x, dim, count):
    before, after = (x.shape[:dim], x.shape[dim + 1 :])
    return jnp.moveaxis(x.reshape(*before, count, -1, *after), dim, 0)


def sent_and_summed(x, axis, dim):
    count = lax.axis_size(axis)
    blocks = lax.all_to_all(in_blocks(x, dim, count), axis, 0, 0, tiled=True)
    return jnp.sum(blocks.astype(jnp.float32), axis=0)


def extended(cells, sides, width):
    for axis, dim in sides:
        count = lax.axis_size(axis)
        ends = count - 1
        head = lax.slice_in_dim(cells, 0, width, axis=dim)
        tail = lax.slice_in_dim(cells, cells.shape[dim] - width, cells.shape[dim], axis=dim)
        cells = jnp.concatenate(
            [
                lax.ppermute(tail, axis, [(i, (i + 1) % count) for i in range(ends)]),
                cells,
                lax.ppermute(head, axis, [((i + 1) % count, i) for i in range(ends)]),
            ],
            axis=dim,
        )
    return cells


def phase_tables(bin_first, bin_count, time_count):
    bin_index = bin_first + jnp.arange(bin_count, dtype=jnp.int32)
    time_index = jnp.arange(time_count, dtype=jnp.int32)
    product = time_index[:, None] * bin_index[None, :] % LEN
    phase_angle = product.astype(jnp.float32) * (2.0 * math.pi / LEN)
    return (jnp.cos(phase_angle), jnp.sin(phase_angle))


def contract(spectrum, operator):
    return jnp.einsum("bsr,bsp->brp", spectrum, operator, preferred_element_type=jnp.float32)


def local(series, kernel, prior_spectrum, prior_scale):
    highest = lax.Precision.HIGHEST
    groups = lax.axis_size("freq")
    first_bin = lax.axis_index("freq") * FB_DEV
    probes, sens_dev, time_dev = series.shape
    total_times = time_dev * groups
    cosine, sine_part = phase_tables(first_bin, FB_DEV, total_times)
    phase_table = jnp.concatenate([cosine, -sine_part], axis=1)
    series_piece = gather_directly(series, "freq", 2)
    row_count = series_piece.shape[2]
    flat_rows = series_piece.astype(jnp.float32).reshape(-1, row_count)
    spectra = jnp.dot(flat_rows, phase_table, precision=highest)
    spectra = (spectra * (1.0 / math.sqrt(total_times))).astype(jnp.bfloat16)
    both_parts = (
        spectra.reshape(probes, sens_dev, 2, FB_DEV)
        .transpose(3, 1, 2, 0)
        .reshape(FB_DEV, sens_dev, 2 * probes)
    )
    with_real = contract(both_parts, kernel[0])
    with_imag = contract(both_parts, kernel[1])
    real_part = with_real[:, :probes] + with_imag[:, probes:]
    imag_part = with_real[:, probes:] - with_imag[:, :probes]
    partial_value = jnp.stack([real_part, imag_part])
    summed = sent_and_summed(partial_value.astype(jnp.bfloat16), "sens", 2)
    weights = prior_spectrum * (1.0 / math.sqrt(FB_DEV * groups))
    scaled_spec = summed * weights[None, :, None, None]
    arrived = lax.all_to_all(scaled_spec, "freq", split_axis=3, concat_axis=1, tiled=True)
    bin_total = arrived.shape[1]
    item_count = arrived.shape[2]
    col_count = arrived.shape[3]
    cos_all, sin_all = phase_tables(0, bin_total, total_times)
    full_table = jnp.concatenate([cos_all, -sin_all], axis=1)
    flat_rows = arrived.reshape(2 * bin_total, item_count * col_count)
    arranged = jnp.dot(full_table, flat_rows, precision=highest).reshape(
        total_times, item_count, col_count
    )
    image_field = lax.all_to_all(arranged, "freq", split_axis=0, concat_axis=2, tiled=True)
    weighted = image_field * prior_scale
    padded = extended(weighted.astype(jnp.bfloat16), (("param", 2),), 1).astype(weighted.dtype)
    smooth = 0.5 * weighted + 0.25 * (padded[:, :, :-2] + padded[:, :, 2:])
    return smooth * prior_scale


def solution(mesh):
    placed = (P(None, "sens", "freq"), P(None, "freq", "sens", "param"), P("freq"), P("param"))
    return jax.shard_map(
        local, mesh=mesh, in_specs=placed, out_specs=P("freq", "sens", "param"), check_vma=False
    )
```

profile of v0, /device:TPU:1, one launch (start us, length us, event | category | flops | bytes accessed | tf_op | source)
XLA Modules:
  0.0 131.3 jit_solution(14938299021006991970)
XLA Ops:
  0.0 2.2 %broadcast_in_dim.2 = bf16[16,8,150,26]{2,1,3,0:T(8,128)(2,1)} broadcast(bf16[8,150,26]{1,0,2:T(8,128)(2,1)} %param.4), dimensions={1,2,3} | broadcast | bytes 1060800 | tf_op jit(solution)/shard_map/broadcast_in_dim | solution.py:19
  2.2 7.6 %all-to-all-start = ((bf16[16,8,150,26]{2,1,3,0:T(8,128)(2,1)}), bf16[16,8,150,26]{2,1,3,0:T(8,128)(2,1)S(1)}, u32[]{:S(2)}, u32[]{:S(2)}) async-start(bf16[16,8,150,26]{2,1,3,0:T(8,128)(2,1)} %broadcast_in_dim.2), calls=%async_computation | async-start | bytes 3407872 | tf_op jit(solution)/shard_map/all_to_all | solution.py:20
  10.0 9.9 %fusion.33 = (bf16[1,16,150,1024]{3,1,2,0:T(8,128)(2,1)}, bf16[1,16,150,1024]{3,1,2,0:T(8,128)(2,1)}) fusion(bf16[2,16,150,1024]{3,1,2,0:T(8,128)(2,1)} %param.5), kind=kLoop, calls=%fused_computation.53 | loop fusion | bytes 19660800 | tf_op jit(solution)/shard_map/slice | solution.py:85
  20.0 14.8 %all-to-all-done = bf16[16,8,150,26]{2,1,3,0:T(8,128)(2,1)S(1)} async-done(((bf16[16,8,150,26]{2,1,3,0:T(8,128)(2,1)}), bf16[16,8,150,26]{2,1,3,0:T(8,128)(2,1)S(1)}, u32[]{:S(2)}, u32[]{:S(2)}) %all-to-all-start) | async-done | bytes 998432 | tf_op jit(solution)/shard_map/all_to_all | solution.py:20
  34.8 1.9 %reshape.30 = bf16[1200,416]{0,1:T(8,128)(2,1)S(1)} reshape(bf16[8,150,16,26]{1,0,3,2:T(8,128)(2,1)S(1)} %bitcast.47) | data formatting | bytes 1996800 | tf_op jit(solution)/shard_map/reshape | solution.py:77
  36.8 0.5 fusion.3
  37.5 8.0 %fusion.1 = f32[16,16,1024]{2,1,0:T(8,128)S(1)} fusion(bf16[1,16,150,1024]{3,1,2,0:T(8,128)(2,1)} %get-tuple-element.5, bf16[8,150,2,16]{1,0,3,2:T(8,128)(2,1)S(1)} %reshape.31), kind=kOutput, calls=%fused_computation.3 | convolution fusion | flops 78643200 | bytes 6040576 | tf_op jit(solution)/shard_map/bsr,bsp->brp/dot_general | solution.py:64
  45.5 5.4 %fusion = f32[16,16,1024]{2,1,0:T(8,128)S(1)} fusion(bf16[1,16,150,1024]{3,1,2,0:T(8,128)(2,1)S(1)} %copy-done, bf16[8,150,2,16]{1,0,3,2:T(8,128)(2,1)S(1)} %reshape.31), kind=kOutput, calls=%fused_computation.1 | convolution fusion | flops 78643200 | bytes 6040576 | tf_op jit(solution)/shard_map/bsr,bsp->brp/dot_general | solution.py:64
  51.2 0.3 stack.9
  51.6 1.3 %copy_bitcast_fusion.4 = bf16[4,2,16,2,1024]{4,3,2,1,0:T(2,128)(2,1)} fusion(bf16[1,16,4,2,1024]{4,3,2,1,0:T(2,128)(2,1)S(1)} %stack.10, bf16[1,16,4,2,1024]{4,3,2,1,0:T(2,128)(2,1)S(1)} %stack.9), kind=kLoop, calls=%fused_computation.18 | loop fusion | flops 262144 | bytes 1048576 | tf_op jit(solution)/shard_map/transpose | solution.py:29
  52.9 5.6 %all-to-all-start.1 = ((bf16[4,2,16,2,1024]{4,3,2,1,0:T(2,128)(2,1)}), bf16[4,2,16,2,1024]{4,3,2,1,0:T(2,128)(2,1)S(1)}, u32[]{:S(2)}, u32[]{:S(2)}) async-start(bf16[4,2,16,2,1024]{4,3,2,1,0:T(2,128)(2,1)} %copy_bitcast_fusion.4), calls=%async_computation.1 | async-start | bytes 1048576 | tf_op jit(solution)/shard_map/all_to_all | solution.py:34
  58.5 13.3 %all-to-all-done.1 = bf16[4,2,16,2,1024]{4,3,2,1,0:T(2,128)(2,1)S(1)} async-done(((bf16[4,2,16,2,1024]{4,3,2,1,0:T(2,128)(2,1)}), bf16[4,2,16,2,1024]{4,3,2,1,0:T(2,128)(2,1)S(1)}, u32[]{:S(2)}, u32[]{:S(2)}) %all-to-all-start.1) | async-done | bytes 524320 | tf_op jit(solution)/shard_map/all_to_all | solution.py:34
  72.0 1.3 %copy.43 = f32[2,16,2,1024]{1,2,0,3:T(2,128)S(1)} copy(f32[2,16,2,1024]{3,1,2,0:T(8,128)S(1)} %broadcast_multiply_fusion) | data formatting | bytes 524288 | tf_op jit(solution)/shard_map/mul | solution.py:92
  73.3 3.6 %reshape.35 = f32[16,1,4096]{2,1,0:T(1,128)} reshape(f32[1024,2,2,16]{3,2,1,0:T(2,128)S(1)} %bitcast.46) | data formatting | bytes 524288
  76.9 5.1 %all-to-all-start.2 = ((f32[16,1,4096]{2,1,0:T(1,128)}), f32[16,1,4096]{2,1,0:T(1,128)S(1)}, u32[]{:S(2)}, u32[]{:S(2)}) async-start(f32[16,1,4096]{2,1,0:T(1,128)} %reshape.35), calls=%async_computation.2 | async-start | bytes 524288 | tf_op jit(solution)/shard_map/all_to_all | solution.py:93
  82.1 1.8 %sine_negate_fusion = (f32[416,256]{1,0:T(8,128)S(1)}, f32[416,256]{1,0:T(8,128)S(1)}) fusion(), kind=kLoop, calls=%fused_computation.21 | loop fusion | flops 1064960 | bytes 851968 | tf_op jit(solution)/shard_map/neg | solution.py:98
  83.9 5.9 %all-to-all-done.2 = f32[16,1,4096]{2,1,0:T(1,128)S(1)} async-done(((f32[16,1,4096]{2,1,0:T(1,128)}), f32[16,1,4096]{2,1,0:T(1,128)S(1)}, u32[]{:S(2)}, u32[]{:S(2)}) %all-to-all-start.2) | async-done | bytes 262176 | tf_op jit(solution)/shard_map/all_to_all | solution.py:93
  89.7 0.5 broadcast.17
  90.2 1.3 reduce
  91.5 2.8 %reshape.36 = f32[1024,2,2,16]{3,2,1,0:T(2,128)S(1)} reshape(f32[16,4096]{1,0:T(8,128)S(1)} %reduce) | data formatting | bytes 524288
  94.3 1.5 %copy.50 = f32[2,16,2,16,64]{4,3,1,2,0:T(8,128)S(1)} copy(f32[2,16,2,16,64]{1,2,0,4,3:T(2,128)S(1)} %bitcast.45) | data formatting | bytes 524288 | tf_op jit(solution)/shard_map/all_to_all | solution.py:93
  95.9 0.4 copy.45
  96.3 0.3 reshape.33
  96.7 0.9 fusion.4
  97.9 0.4 reshape.37
  98.3 10.1 %all_to_all.43 = f32[16,1,3328]{2,1,0:T(1,128)S(1)} all-to-all(f32[16,1,3328]{2,1,0:T(1,128)S(1)} %reshape.37), channel_id=1, replica_groups=mesh['freq'=16,'param'=4,'sens'=4] {'freq'}, dimensions={0} | all-to-all | bytes 425984 | tf_op jit(solution)/shard_map/all_to_all | solution.py:103
  108.4 1.1 reduce.1
  110.3 10.5 %collective-permute-start = (bf16[26,2,1]{2,1,0:T(2,128)(2,1)S(1)}, bf16[26,2,1]{2,1,0:T(2,128)(2,1)S(1)}, u32[]{:S(2)}, u32[]{:S(2)}) collective-permute-start(bf16[26,2,1]{2,1,0:T(2,128)(2,1)S(1)} %get-tuple-element.10), channel_id=1, source_target_pairs={{0,4},{4,8},{8,12},{1,5},{5,9},{9,13},{2,6},{6,10},{10,14},{3,7},{... | collective-permute-start | bytes 320 | tf_op jit(solution)/shard_map/ppermute | solution.py:46
  120.8 1.9 %collective-permute-start.1 = (bf16[26,2,1]{2,1,0:T(2,128)(2,1)S(1)}, bf16[26,2,1]{2,1,0:T(2,128)(2,1)S(1)}, u32[]{:S(2)}, u32[]{:S(2)}) collective-permute-start(bf16[26,2,1]{2,1,0:T(2,128)(2,1)S(1)} %get-tuple-element.9), channel_id=1, source_target_pairs={{4,0},{8,4},{12,8},{5,1},{9,5},{13,9},{6,2},{10,6},{14,10},{7,3},{... | collective-permute-start | bytes 320 | tf_op jit(solution)/shard_map/ppermute | solution.py:48
  122.8 7.0 %collective-permute-done.1 = bf16[26,2,1]{2,1,0:T(2,128)(2,1)S(1)} collective-permute-done((bf16[26,2,1]{2,1,0:T(2,128)(2,1)S(1)}, bf16[26,2,1]{2,1,0:T(2,128)(2,1)S(1)}, u32[]{:S(2)}, u32[]{:S(2)}) %collective-permute-start.1) | collective-permute-done | bytes 136 | tf_op jit(solution)/shard_map/ppermute | solution.py:48
  129.8 0.5 concatenate.13
  130.3 1.0 fusion.17
  (23 shorter events, 2.1 us)
Async XLA Ops:
  2.2 32.6 %all-to-all-start = ((bf16[16,8,150,26]{2,1,3,0:T(8,128)(2,1)}), bf16[16,8,150,26]{2,1,3,0:T(8,128)(2,1)S(1)}, u32[]{:S(2)}, u32[]{:S(2)}) async-start(bf16[16,8,150,26]{2,1,3,0:T(8,128)(2,1)} %broadcast_in_dim.2), calls=%async_computation | async-start | bytes 3407872 | tf_op jit(solution)/shard_map/all_to_all | solution.py:20
  37.5 8.0 %copy-start = (bf16[1,16,150,1024]{3,1,2,0:T(8,128)(2,1)S(1)}, bf16[1,16,150,1024]{3,1,2,0:T(8,128)(2,1)}, u32[]{:S(2)}) copy-start(bf16[1,16,150,1024]{3,1,2,0:T(8,128)(2,1)} %get-tuple-element.6) | copy-start | bytes 14745604
  45.5 13.0 %copy-start.2 = (f32[16]{0:T(128)S(1)}, f32[16]{0:T(128)}, u32[]{:S(2)}) copy-start(f32[16]{0:T(128)} %param.6) | copy-start | bytes 196
  52.9 18.9 %all-to-all-start.1 = ((bf16[4,2,16,2,1024]{4,3,2,1,0:T(2,128)(2,1)}), bf16[4,2,16,2,1024]{4,3,2,1,0:T(2,128)(2,1)S(1)}, u32[]{:S(2)}, u32[]{:S(2)}) async-start(bf16[4,2,16,2,1024]{4,3,2,1,0:T(2,128)(2,1)} %copy_bitcast_fusion.4), calls=%async_computation.1 | async-start | bytes 1048576 | tf_op jit(solution)/shard_map/all_to_all | solution.py:34
  76.9 12.8 %all-to-all-start.2 = ((f32[16,1,4096]{2,1,0:T(1,128)}), f32[16,1,4096]{2,1,0:T(1,128)S(1)}, u32[]{:S(2)}, u32[]{:S(2)}) async-start(f32[16,1,4096]{2,1,0:T(1,128)} %reshape.35), calls=%async_computation.2 | async-start | bytes 524288 | tf_op jit(solution)/shard_map/all_to_all | solution.py:93
  94.3 15.8 %copy-start.1 = (f32[1024]{0:T(1024)S(1)}, f32[1024]{0:T(1024)}, u32[]{:S(2)}) copy-start(f32[1024]{0:T(1024)} %param.7) | copy-start | bytes 12292
  110.3 12.4 %collective-permute-start = (bf16[26,2,1]{2,1,0:T(2,128)(2,1)S(1)}, bf16[26,2,1]{2,1,0:T(2,128)(2,1)S(1)}, u32[]{:S(2)}, u32[]{:S(2)}) collective-permute-start(bf16[26,2,1]{2,1,0:T(2,128)(2,1)S(1)} %get-tuple-element.10), channel_id=1, source_target_pairs={{0,4},{4,8},{8,12},{1,5},{5,9},{9,13},{2,6},{6,10},{10,14},{3,7},{... | collective-permute-start | bytes 320 | tf_op jit(solution)/shard_map/ppermute | solution.py:46
  120.8 8.9 %collective-permute-start.1 = (bf16[26,2,1]{2,1,0:T(2,128)(2,1)S(1)}, bf16[26,2,1]{2,1,0:T(2,128)(2,1)S(1)}, u32[]{:S(2)}, u32[]{:S(2)}) collective-permute-start(bf16[26,2,1]{2,1,0:T(2,128)(2,1)S(1)} %get-tuple-element.9), channel_id=1, source_target_pairs={{4,0},{8,4},{12,8},{5,1},{9,5},{13,9},{6,2},{10,6},{14,10},{7,3},{... | collective-permute-start | bytes 320 | tf_op jit(solution)/shard_map/ppermute | solution.py:48
where the time goes:
time: 132 us; the launch traced here: 131 us
  waiting for transfers between devices  41 us (31%)
  starting transfers between devices  30.7 us (23%)
  local copies, waits for them, and re-layouts  27.1 us (21%)
  matrix products  14.8 us (11%)
  blocking collectives  10.1 us (8%)
  other arithmetic  7.26 us (6%)
    all_to_all x1, waiting for transfers between devices, copy_for_each(): return lax.all_to_all(copies, axis, split_axis=0, concat_axis=0, tiled=True)  14.8 us
    dot_general x2, matrix products, contract(): jnp.einsum('bsr,bsp->brp', spectrum, operator, preferred_element_type=jnp...  13.4 us
    all_to_all x1, waiting for transfers between devices, sent_and_summed(): blocks = lax.all_to_all(in_blocks(x, dim, count), axis, 0, 0, tiled=True)  13.3 us
    ppermute x1, starting transfers between devices, extended(): lax.ppermute(tail, axis, [(i, (i + 1) % count) for i in range(ends)])  10.5 us
    all_to_all x1, blocking collectives, local(): lax.all_to_all(arranged, 'freq', split_axis=0, concat_axis=2, tiled=True)  10.1 us
    slice x1, local copies, waits for them, and re-layouts, local(): with_real = contract(both_parts, kernel[0])  9.95 us
    all_to_all x1, starting transfers between devices, copy_for_each(): return lax.all_to_all(copies, axis, split_axis=0, concat_axis=0, tiled=True)  7.57 us
    unnamed x10, local copies, waits for them, and re-layouts  7.13 us
  transfers between devices with their start and end apart: 5, of which 4 were waited for; matrix products, arithmetic and copies ran while one was open for 9% of the time, Pallas kernels for 0%

commit v1 on v0

v1 whole, which is shorter than its diff:
```python
import functools
import math

import jax
import jax.numpy as jnp
from jax import lax
from jax.experimental import pallas as pl
from jax.experimental.pallas import tpu as pltpu
from jax.sharding import PartitionSpec as P

LEN = 840
MESH = pl.DeviceIdType.MESH
F32, BF16 = jnp.float32, jnp.bfloat16
CHUNKS = ((0, 7), (1, 2), (3, 4), (5, 6))
READY = ((), (0, 1), (2, 3), (4, 5, 6, 7))


def iota(shape, dim):
    return lax.broadcasted_iota(jnp.int32, shape, dim)


def turned_cos(bins, times, part):
    turn = bins.astype(F32) * times.astype(F32) + (LEN // 4) * part.astype(F32)
    turn = turn - LEN * jnp.floor(turn * (1.0 / LEN) + 0.5)
    half = turn * (math.pi / LEN)
    square = half * half
    term = 1.0 / 6227020800.0
    for coef in (-1.0 / 39916800.0, 1.0 / 362880.0, -1.0 / 5040.0, 1.0 / 120.0, -1.0 / 6.0, 1.0):
        term = term * square + coef
    sine = half * term
    return 1.0 - 2.0 * sine * sine


def split(x):
    high = x.astype(BF16)
    return high, (x - high.astype(F32)).astype(BF16)


def kernel(
    series_ref, kern_ref, prior_ref, scale_ref, out_ref,
    ser_v, kern_v, by_time, turned, arecv, bsend, brecv, packed, lhs_re, lhs_im, zsend, zrecv, zfull,
    hsend, hrecv, wsend, wrecv, isend, irecv, table_hi, table_lo,
    local_sem, send_sem, recv_sem, zsend_sem, zrecv_sem, hsend_sem, hrecv_sem,
):
    f, par, s = lax.axis_index("freq"), lax.axis_index("param"), lax.axis_index("sens")
    y, x = f // 4, f % 4
    core = par % 2
    sensors = ser_v.shape[2]
    row = kern_v.shape[4] // 128
    rest_of = sensors - 128
    first_at = lambda j: j * (1 + 3 * core) + 4 * y * (1 - core) + x * core
    second_at = lambda m: m * (4 - 3 * core) + x * (1 - core) + 4 * y * core
    first_pos = x * (1 - core) + y * core
    second_pos = y * (1 - core) + x * core

    series_in = pltpu.make_async_copy(series_ref, ser_v, local_sem.at[0])
    series_in.start()
    kernel_in = []
    for p in range(2):
        for h in range(2):
            kernel_in.append(
                pltpu.make_async_copy(
                    kern_ref.at[p, :, pl.ds(8 * h, 8)], kern_v.at[h, p], local_sem.at[1 + 2 * h + p]
                )
            )
            kernel_in[-1].start()

    barrier = pltpu.get_barrier_semaphore()
    for o in range(1, 16):
        pl.semaphore_signal(barrier, 1, device_id={"freq": (f + o) % 16}, device_id_type=MESH)
    for o in range(1, 4):
        pl.semaphore_signal(barrier, 1, device_id={"sens": (s + o) % 4}, device_id_type=MESH)
    other = par + 1 - 2 * core
    for m in range(4):
        source = m * (1 + 3 * core) + 4 * y * (1 - core) + x * core
        pl.semaphore_signal(barrier, 1, device_id={"freq": source, "param": other}, device_id_type=MESH)

    @pl.when(par == 1)
    def _():
        pl.semaphore_signal(barrier, 1, device_id={"param": 2}, device_id_type=MESH)

    @pl.when(par == 2)
    def _():
        pl.semaphore_signal(barrier, 1, device_id={"param": 1}, device_id_type=MESH)

    ri, ci = iota((128, 128), 0), iota((128, 128), 1)
    bins = 16 * second_at(ri >> 5) + (ri & 15)
    inside = ci & 31
    times = 26 * first_at(ci >> 5) + inside
    forward = jnp.where(inside < 26, turned_cos(bins, times, (ri >> 4) & 1), 0.0)
    fwd_hi, fwd_lo = split(forward)

    turned[:, 512:640] = jnp.zeros((32, 128), F32)
    turned[24:32, :] = jnp.zeros((8, 640), F32)
    series_in.wait()
    by_time[0] = ser_v[:, :, 0:128].astype(F32).reshape(208, 128)
    by_time[1, :, 0:rest_of] = ser_v[:, :, 128:sensors].astype(F32).reshape(208, rest_of)
    for i in range(4):
        rows = pl.ds(4 * core + i, 26, stride=8)
        turned[0:26, 128 * i : 128 * i + 128] = by_time[0, rows, :]
        turned[0:26, 512 + 32 * i : 512 + 32 * i + rest_of] = by_time[1, rows, :][:, 0:rest_of]
    arecv[first_pos] = turned[...].astype(BF16)

    pl.semaphore_wait(barrier, 22 + jnp.where((par == 1) | (par == 2), 1, 0))

    for o in range(1, 4):
        pltpu.make_async_remote_copy(
            arecv.at[first_pos], arecv.at[first_pos], send_sem.at[0], recv_sem.at[0],
            device_id={"freq": first_at((first_pos + o) % 4)}, device_id_type=MESH,
        ).start()

    @pl.loop(0, 16)
    def _(b):
        ti, ki = iota((32, 512), 0), iota((32, 512), 1)
        values = turned_cos(((ki >> 5) << 4) + ((ki >> 4) & 1) * 8 + (ki & 7), 26 * b + ti, (ki >> 3) & 1)
        high, low = split(values)
        rows = pl.ds(pl.multiple_of(32 * b, 32), 32)
        table_hi[rows, :] = high
        table_lo[rows, :] = low

    def drain(like, sem):
        pltpu.make_async_copy(like, like, sem).wait()

    drain(arecv.at[pl.ds(0, 3)], recv_sem.at[0])
    gathered = arecv[...].reshape(128, 640)
    spec = jnp.dot(fwd_hi, gathered, preferred_element_type=F32)
    spec = spec + jnp.dot(fwd_lo, gathered, preferred_element_type=F32)
    spec = spec * (1.0 / math.sqrt(416.0))
    bsend[...] = spec.astype(BF16).reshape(4, 32, 640)
    for o in range(4):
        m = (second_pos + o) % 4
        for c in range(2):
            if o + c > 0:
                target = par + (1 - 2 * core) * c
                pltpu.make_async_remote_copy(
                    bsend.at[m], brecv.at[4 * core + second_pos], send_sem.at[1], recv_sem.at[1],
                    device_id={"freq": second_at(m), "param": target}, device_id_type=MESH,
                ).start()
    brecv[4 * core + second_pos] = bsend[second_pos]
    drain(brecv.at[pl.ds(0, 7)], recv_sem.at[1])

    lane = iota((32, 128), 1)
    for c in range(2):
        total = brecv[4 * c].astype(F32)
        for m in range(1, 4):
            total = total + brecv[4 * c + m].astype(F32)
        rest = total[:, 512:640]
        for i in range(4):
            tail = rest if i == 0 else pltpu.roll(rest, 128 - 32 * i, 1)
            tail = jnp.where(lane < 32, tail, 0.0)
            wide = jnp.concatenate([total[:, 128 * i : 128 * i + 128], tail], axis=1)
            for h in range(2):
                pair = [wide[16 * p + 8 * h : 16 * p + 8 * h + 8] for p in range(2)]
                packed[h, pl.ds(16 * (4 * c + i), 16), :] = jnp.concatenate(pair, axis=0).astype(BF16)
    width = 8 * sensors
    compact = packed[...].reshape(256, 256)[:, 0:sensors]
    diagonal = iota((16, 256), 0) % 8 == iota((16, 256), 1) % 8
    for at in range(0, width, 256):
        size = min(256, width - at)
        spread = (iota((sensors, size), 0) == (at + iota((sensors, size), 1)) // 8).astype(BF16)
        spaced = jnp.dot(compact, spread, preferred_element_type=F32)
        for r in range(16):
            block = jnp.where(diagonal[:, 0:size], spaced[16 * r : 16 * r + 16], 0.0)
            rows = slice(16 * (r % 8), 16 * (r % 8) + 16)
            lhs_re[r // 8, rows, at : at + size] = block.astype(BF16)
            turned_block = jnp.concatenate([block[8:16], -block[0:8]], axis=0)
            lhs_im[r // 8, rows, at : at + size] = turned_block.astype(BF16)

    for copy in kernel_in:
        copy.wait()

    def lanes(tile, count=1):
        return slice(128 * tile, 128 * (tile + count))

    eighth = iota((8, 256), 0)
    weights = []
    for h in range(2):
        column = jnp.zeros((8, 256), F32)
        for k in range(8):
            column = jnp.where(eighth == k, prior_ref[8 * h + k] * (1.0 / 16.0), column)
        weights.append(column)

    for n, (left, right) in enumerate(CHUNKS):
        scale = jnp.concatenate([scale_ref[:, lanes(left)], scale_ref[:, lanes(right)]], axis=1)
        for h in range(2):
            product = jnp.zeros((128, 256), F32)
            for p, lhs in ((0, lhs_re), (1, lhs_im)):
                operand = jnp.concatenate(
                    [kern_v[h, p, :, :, lanes(left)], kern_v[h, p, :, :, lanes(right)]], axis=2
                ).reshape(width, 256)
                product = product + jnp.dot(lhs[h, :, 0:width], operand, preferred_element_type=F32)
            factor = jnp.concatenate([weights[h] * scale] * 4, axis=0)
            for d in range(4):
                zsend[n, d, pl.ds(32 * h, 32), :] = (product[32 * d : 32 * d + 32] * factor).astype(BF16)
        for o in range(1, 4):
            target = (s + o) % 4
            pltpu.make_async_remote_copy(
                zsend.at[n, target], zrecv.at[n, s], zsend_sem.at[n], zrecv_sem.at[n],
                device_id={"sens": target}, device_id_type=MESH,
            ).start()

    @pl.when(par == 0)
    def _():
        hrecv[0] = jnp.zeros((8, 128), F32)

    @pl.when(par == 3)
    def _():
        hrecv[1] = jnp.zeros((8, 128), F32)

    lane = iota((8, 128), 1)
    lane64 = iota((64, 128), 1)
    for n, (left, right) in enumerate(CHUNKS):
        drain(zrecv.at[n, pl.ds(0, 3)], zrecv_sem.at[n])
        total = zsend[n, s].astype(F32)
        for o in range(1, 4):
            total = total + zrecv[n, (s + o) % 4].astype(F32)
        zfull[:, lanes(left + 1)] = total[:, 0:128]
        zfull[:, lanes(right + 1)] = total[:, 128:256]
        if n == 0:
            for e, piece in ((0, total[:, 0:128]), (1, total[:, 128:256])):
                columns = jnp.zeros((8, 128), F32)
                for j in range(8):
                    shift = j + e
                    block = piece[8 * j : 8 * j + 8]
                    moved = block if shift == 0 else pltpu.roll(block, shift, 1)
                    columns = jnp.where(lane == j, moved, columns)
                hsend[e] = columns

            @pl.when(par > 0)
            def _():
                pltpu.make_async_remote_copy(
                    hsend.at[0], hrecv.at[1], hsend_sem.at[0], hrecv_sem.at[1],
                    device_id={"param": par - 1}, device_id_type=MESH,
                ).start()

            @pl.when(par < 3)
            def _():
                pltpu.make_async_remote_copy(
                    hsend.at[1], hrecv.at[0], hsend_sem.at[1], hrecv_sem.at[0],
                    device_id={"param": par + 1}, device_id_type=MESH,
                ).start()

        for t in READY[n]:
            if t == 0 or t == row - 1:
                e = 0 if t == 0 else 1

                @pl.when(par > 0 if e == 0 else par < 3)
                def _(e=e):
                    drain(hrecv.at[e], hrecv_sem.at[e])

                edge = hrecv[e]
                for j in range(8):
                    shift = 127 - j if e == 0 else (128 - j) % 128
                    moved = edge if shift == 0 else pltpu.roll(edge, shift, 1)
                    zfull[8 * j : 8 * j + 8, lanes(0 if e == 0 else row + 1)] = moved
            before, here, after = (zfull[:, lanes(t + i)] for i in range(3))
            low = jnp.where(lane64 == 0, pltpu.roll(before, 1, 1), pltpu.roll(here, 1, 1))
            high = jnp.where(lane64 == 127, pltpu.roll(after, 127, 1), pltpu.roll(here, 127, 1))
            smooth = (0.5 * here + 0.25 * (low + high)) * scale_ref[:, lanes(t)]
            for q in range(2):
                owner = 8 * q + t
                halves = [smooth[32 * h + 16 * q : 32 * h + 16 * q + 16] for h in range(2)]
                wsend[t, q] = jnp.concatenate(halves, axis=0).astype(BF16)
                piece = wsend.at[t, q]

                @pl.when(f != owner)
                def _(owner=owner, piece=piece):
                    pltpu.make_async_remote_copy(
                        piece, wrecv.at[f], send_sem.at[2], recv_sem.at[2],
                        device_id={"freq": owner}, device_id_type=MESH,
                    ).start()

                @pl.when(f == owner)
                def _(piece=piece):
                    pltpu.make_async_copy(piece, wrecv.at[f], recv_sem.at[2]).start()

    drain(wrecv, recv_sem.at[2])
    spectra = wrecv[...].reshape(512, 128)
    image = jnp.dot(table_hi[...], spectra, preferred_element_type=F32)
    image = image + jnp.dot(table_lo[...], spectra, preferred_element_type=F32)
    isend[...] = image.astype(BF16).reshape(16, 32, 128)
    for o in range(1, 16):
        target = (f + o) % 16
        pltpu.make_async_remote_copy(
            isend.at[target], irecv.at[f], send_sem.at[3], recv_sem.at[3],
            device_id={"freq": target}, device_id_type=MESH,
        ).start()
    irecv[f] = isend[f]

    drain(arecv.at[pl.ds(0, 3)], send_sem.at[0])
    drain(brecv.at[pl.ds(0, 7)], send_sem.at[1])
    for n in range(4):
        drain(zrecv.at[n, pl.ds(0, 3)], zsend_sem.at[n])

    @pl.when(par > 0)
    def _():
        drain(hsend.at[0], hsend_sem.at[0])

    @pl.when(par < 3)
    def _():
        drain(hsend.at[1], hsend_sem.at[1])

    drain(wrecv.at[pl.ds(0, 15)], send_sem.at[2])
    drain(isend.at[pl.ds(0, 15)], send_sem.at[3])
    drain(irecv.at[pl.ds(0, 15)], recv_sem.at[3])
    out_ref[...] = irecv[...]


def local(series, kern, prior_spectrum, prior_scale):
    sensors, params = kern.shape[2:]
    series, kern = series.transpose(2, 0, 1), kern.transpose(0, 2, 1, 3)
    vmem = pltpu.VMEM
    dma = pltpu.SemaphoreType.DMA
    image = pl.pallas_call(
        kernel,
        out_shape=jax.ShapeDtypeStruct((16, 32, 128), BF16),
        in_specs=[
            pl.BlockSpec(memory_space=pl.ANY),
            pl.BlockSpec(memory_space=pl.ANY),
            pl.BlockSpec(memory_space=pltpu.SMEM),
            pl.BlockSpec(memory_space=pltpu.VMEM),
        ],
        out_specs=pl.BlockSpec(memory_space=pltpu.VMEM),
        scratch_shapes=[
            vmem((26, 8, sensors), BF16),
            vmem((2, 2, sensors, 8, params), BF16),
            vmem((2, 208, 128), F32),
            vmem((32, 640), F32),
            vmem((4, 32, 640), BF16),
            vmem((4, 32, 640), BF16),
            vmem((8, 32, 640), BF16),
            vmem((2, 128, 256), BF16),
            vmem((2, 128, 8 * sensors), BF16),
            vmem((2, 128, 8 * sensors), BF16),
            vmem((4, 4, 64, 256), BF16),
            vmem((4, 4, 64, 256), BF16),
            vmem((64, 1280), F32),
            vmem((2, 8, 128), F32),
            vmem((2, 8, 128), F32),
            vmem((8, 2, 32, 128), BF16),
            vmem((16, 32, 128), BF16),
            vmem((16, 32, 128), BF16),
            vmem((16, 32, 128), BF16),
            vmem((512, 512), BF16),
            vmem((512, 512), BF16),
            dma((5,)),
            dma((4,)),
            dma((4,)),
            dma((4,)),
            dma((4,)),
            dma((2,)),
            dma((2,)),
        ],
        compiler_params=pltpu.CompilerParams(
            collective_id=0, has_side_effects=True, vmem_limit_bytes=60 * 1024 * 1024
        ),
        name="adjoint",
    )(series, kern, prior_spectrum, prior_scale.reshape(1, -1))
    image = image.reshape(2, 8, 32, 128)[:, :, :26].astype(F32)
    return image.transpose(2, 0, 1, 3).reshape(26, 2, params)


def solution(mesh):
    placed = (P(None, "sens", "freq"), P(None, "freq", "sens", "param"), P("freq"), P("param"))
    return jax.shard_map(
        local, mesh=mesh, in_specs=placed, out_specs=P("freq", "sens", "param"), check_vma=False
    )
```

time: 132 us -> 45.2 us (0.34)
  the two profiles are of different devices: /device:TPU:1 before, /device:TPU:32 now
where the time goes in v1:
time: 45.2 us; the launch traced here: 44.5 us
  Pallas kernels  42.7 us (94%)
  other arithmetic  0.92 us (2%)
  local copies, waits for them, and re-layouts  0.92 us (2%)
    pallas_call x1, Pallas kernels, local(): pl.pallas_call(kernel, out_shape=jax.ShapeDtypeStruct((16, 32, 128), BF16...  42.7 us
    reshape x1, other arithmetic, local(): return image.transpose(2, 0, 1, 3).reshape(26, 2, params)  0.92 us
    reshape x2, local copies, waits for them, and re-layouts, local(): return image.transpose(2, 0, 1, 3).reshape(26, 2, params)  0.92 us

profile of v1, /device:TPU:32, one launch (start us, length us, event | category | flops | bytes accessed | tf_op | source)
XLA Modules:
  0.0 44.5 jit_solution(12704892382672457794)
XLA Ops:
  0.0 42.7 %adjoint.1 = bf16[16,32,128]{2,1,0:T(8,128)(2,1)} custom-call(bf16[26,8,150]{2,1,0:T(8,128)(2,1)} %bitcast.10, bf16[2,150,16,1024]{3,2,1,0:T(8,128)(2,1)} %bitcast.8, f32[16]{0:T(128)} %prior_ref.1, f32[1,1024]{1,0:T(1,128)} %bitcast.11), custom_call_target="tpu_custom_call" | custom-call | tf_op jit(solution)/shard_map/adjoint/pallas_call | solution.py:314
  42.7 0.9 %convert_bitcast_fusion = f32[26,2,8,128]{3,0,2,1:T(8,128)S(1)} fusion(bf16[2,8,32,128]{3,2,1,0:T(8,128)(2,1)} %bitcast.9), kind=kLoop, calls=%fused_computation | loop fusion | flops 53248 | bytes 319488 | tf_op jit(solution)/shard_map/reshape | solution.py:360
  43.6 0.1 copy.5
  43.7 0.8 %reshape.17 = f32[26,2,1024]{2,1,0:T(2,128)} reshape(f32[26,2,8,128]{3,2,1,0:T(8,128)S(1)} %copy.5) | data formatting | bytes 425984 | tf_op jit(solution)/shard_map/reshape | solution.py:360

commit v2 on v1

v2 whole, which is shorter than its diff:
```python
import functools
import math

import jax
import jax.numpy as jnp
from jax import lax
from jax.experimental import pallas as pl
from jax.experimental.pallas import tpu as pltpu
from jax.sharding import PartitionSpec as P

LEN = 840
MESH = pl.DeviceIdType.MESH
F32, BF16 = jnp.float32, jnp.bfloat16
CHUNKS = ((0, 7), (1, 2), (3, 4), (5, 6))
READY = ((), (0, 1), (2, 3), (4, 5, 6, 7))
STEPS = sorted(((i, j) for i in range(4) for j in range(4) if i + j), key=lambda v: -sum(min(a, 4 - a) for a in v))


def owner_of(half, tile):
    early, low = int(tile < 4), tile % 4
    at_y = 2 * half + low // 2
    return 4 * at_y + 2 * (low % 2) + (early + at_y) % 2


def iota(shape, dim):
    return lax.broadcasted_iota(jnp.int32, shape, dim)


def turned_cos(bins, times, part):
    turn = bins.astype(F32) * times.astype(F32) + (LEN // 4) * part.astype(F32)
    turn = turn - LEN * jnp.floor(turn * (1.0 / LEN) + 0.5)
    half = turn * (math.pi / LEN)
    square = half * half
    term = 1.0 / 6227020800.0
    for coef in (-1.0 / 39916800.0, 1.0 / 362880.0, -1.0 / 5040.0, 1.0 / 120.0, -1.0 / 6.0, 1.0):
        term = term * square + coef
    sine = half * term
    return 1.0 - 2.0 * sine * sine


def split(x):
    high = x.astype(BF16)
    return high, (x - high.astype(F32)).astype(BF16)


def kernel(
    series_ref, kern_ref, prior_hbm, scale_hbm, out_ref,
    prior_ref, scale_ref, ser_v, kern_v, by_time, turned, arecv, bsend, brecv, packed, lhs_re, lhs_im, zsend, zpart, zfwd, zrecv, zfull,
    hsend, hrecv, wsend, wrecv, isend, irecv, table_hi, table_lo,
    local_sem, send_sem, recv_sem, zsend_sem, zrecv_sem, hsend_sem, hrecv_sem,
):
    f, par, s = lax.axis_index("freq"), lax.axis_index("param"), lax.axis_index("sens")
    y, x = f // 4, f % 4
    core = par % 2
    sensors = ser_v.shape[2]
    row = kern_v.shape[4] // 128
    rest_of = sensors - 128
    late = 1 - (x + y) % 2
    slot = 8 * (y // 2) + 2 * (y % 2) + x // 2 + 4 * late
    end = (s == 0) | (s == 3)
    middle = (s == 1) | (s == 2)
    near, beyond = 1 + s // 3, 2 - s // 3
    across = 3 - s
    side = jnp.where(end, near, 3 * (s - 1))
    far = jnp.where(end, across, 6 - 3 * s)
    first_at = lambda j: j * (1 + 3 * core) + 4 * y * (1 - core) + x * core
    second_at = lambda m: m * (4 - 3 * core) + x * (1 - core) + 4 * y * core
    first_pos = x * (1 - core) + y * core
    second_pos = y * (1 - core) + x * core

    barrier = pltpu.get_barrier_semaphore()
    for i, j in sorted(STEPS, key=sum):
        peer = 4 * ((y + j) % 4) + (x + i) % 4
        pl.semaphore_signal(barrier, 1, device_id={"freq": peer}, device_id_type=MESH)
    for o in range(1, 4):
        pl.semaphore_signal(barrier, 1, device_id={"sens": (s + o) % 4}, device_id_type=MESH)
    other = par + 1 - 2 * core
    for m in range(4):
        source = m * (1 + 3 * core) + 4 * y * (1 - core) + x * core
        pl.semaphore_signal(barrier, 1, device_id={"freq": source, "param": other}, device_id_type=MESH)

    @pl.when(par == 1)
    def _():
        pl.semaphore_signal(barrier, 1, device_id={"param": 2}, device_id_type=MESH)

    @pl.when(par == 2)
    def _():
        pl.semaphore_signal(barrier, 1, device_id={"param": 1}, device_id_type=MESH)

    series_in = pltpu.make_async_copy(series_ref, ser_v, local_sem.at[0])
    series_in.start()
    small_in = []
    for n, (source, target) in enumerate(((prior_hbm, prior_ref), (scale_hbm, scale_ref))):
        small_in.append(pltpu.make_async_copy(source, target, local_sem.at[5 + n]))
        small_in[-1].start()
    kernel_in = []
    for p in range(2):
        for h in range(2):
            kernel_in.append(
                pltpu.make_async_copy(
                    kern_ref.at[p, :, pl.ds(8 * h, 8)], kern_v.at[h, p], local_sem.at[1 + 2 * h + p]
                )
            )
            kernel_in[-1].start()

    ri, ci = iota((128, 128), 0), iota((128, 128), 1)
    bins = 16 * second_at(ri >> 5) + (ri & 15)
    inside = ci & 31
    times = 26 * first_at(ci >> 5) + inside
    forward = jnp.where(inside < 26, turned_cos(bins, times, (ri >> 4) & 1), 0.0)
    fwd_hi, fwd_lo = split(forward)

    turned[:, 24:32, :] = jnp.zeros((2, 8, 384), F32)
    turned[:, :, 256:384] = jnp.zeros((2, 32, 128), F32)
    series_in.wait()
    by_time[0] = ser_v[:, :, 0:128].astype(F32).reshape(208, 128)
    by_time[1, :, 0:rest_of] = ser_v[:, :, 128:sensors].astype(F32).reshape(208, rest_of)
    for g in range(2):
        for q in range(2):
            rows = pl.ds((6 * core if g == 0 else 2 + 2 * core) + q, 26, stride=8)
            turned[g, 0:26, 128 * q : 128 * q + 128] = by_time[0, rows, :]
            turned[g, 0:26, 256 + 32 * q : 256 + 32 * q + rest_of] = by_time[1, rows, :][:, 0:rest_of]
        arecv[g, first_pos] = turned[g].astype(BF16)

    pl.semaphore_wait(barrier, 22 + jnp.where((par == 1) | (par == 2), 1, 0))

    for g in range(2):
        for o in (2, 1, 3):
            pltpu.make_async_remote_copy(
                arecv.at[g, first_pos], arecv.at[g, first_pos], send_sem.at[g], recv_sem.at[g],
                device_id={"freq": first_at((first_pos + o) % 4)}, device_id_type=MESH,
            ).start()

    @pl.loop(0, 16)
    def _(b):
        ti, ki = iota((32, 512), 0), iota((32, 512), 1)
        owner = 4 * ((y + 2 + b // 4) % 4) + b % 4
        values = turned_cos(((ki >> 5) << 4) + ((ki >> 4) & 1) * 8 + (ki & 7), 26 * owner + ti, (ki >> 3) & 1)
        high, low = split(values)
        rows = pl.ds(pl.multiple_of(32 * b, 32), 32)
        table_hi[rows, :] = high
        table_lo[rows, :] = low

    def drain(like, sem):
        pltpu.make_async_copy(like, like, sem).wait()

    for g in range(2):
        drain(arecv.at[g, pl.ds(0, 3)], recv_sem.at[g])
        gathered = arecv[g].reshape(128, 384)
        spec = jnp.dot(fwd_hi, gathered, preferred_element_type=F32)
        spec = spec + jnp.dot(fwd_lo, gathered, preferred_element_type=F32)
        spec = spec * (1.0 / math.sqrt(416.0))
        bsend[g] = spec.astype(BF16).reshape(4, 32, 384)
        for o in (2, 1, 3, 0):
            m = (second_pos + o) % 4
            for c in range(2):
                if o + c > 0:
                    target = par + (1 - 2 * core) * c
                    pltpu.make_async_remote_copy(
                        bsend.at[g, m], brecv.at[g, 4 * core + second_pos],
                        send_sem.at[2 + g], recv_sem.at[2 + g],
                        device_id={"freq": second_at(m), "param": target}, device_id_type=MESH,
                    ).start()
        brecv[g, 4 * core + second_pos] = bsend[g, second_pos]

    lane = iota((32, 128), 1)
    width = 8 * sensors
    diagonal = iota((16, 256), 0) % 8 == iota((16, 256), 1) % 8

    def spread_out(g):
        for c in range(2):
            total = brecv[g, 4 * c].astype(F32)
            for m in range(1, 4):
                total = total + brecv[g, 4 * c + m].astype(F32)
            for q in range(2):
                tail = total[:, 256:384]
                tail = tail if q == 0 else pltpu.roll(tail, 128 - 32 * q, 1)
                tail = jnp.where(lane < 32, tail, 0.0)
                wide = jnp.concatenate([total[:, 128 * q : 128 * q + 128], tail], axis=1)
                for h in range(2):
                    pair = [wide[16 * p + 8 * h : 16 * p + 8 * h + 8] for p in range(2)]
                    packed[g, h, pl.ds(32 * c + 16 * q, 16), :] = jnp.concatenate(pair, axis=0).astype(BF16)
        compact = packed[g].reshape(128, 256)[:, 0:sensors]
        for at in range(0, width, 256):
            size = min(256, width - at)
            spread = (iota((sensors, size), 0) == (at + iota((sensors, size), 1)) // 8).astype(BF16)
            spaced = jnp.dot(compact, spread, preferred_element_type=F32)
            for r in range(8):
                block = jnp.where(diagonal[:, 0:size], spaced[16 * r : 16 * r + 16], 0.0)
                rows = slice(16 * (r % 4), 16 * (r % 4) + 16)
                lhs_re[g, r // 4, rows, at : at + size] = block.astype(BF16)
                swapped = jnp.concatenate([block[8:16], -block[0:8]], axis=0)
                lhs_im[g, r // 4, rows, at : at + size] = swapped.astype(BF16)

    drain(brecv.at[0, pl.ds(0, 7)], recv_sem.at[2])
    spread_out(0)
    for copy in small_in + kernel_in:
        copy.wait()

    def send_along(source, target, kind, n, received, to):
        pltpu.make_async_remote_copy(
            source, target, zsend_sem.at[4 * kind + n], zrecv_sem.at[received],
            device_id={"sens": to}, device_id_type=MESH,
        ).start()

    def lanes(tile, count=1):
        return slice(128 * tile, 128 * (tile + count))

    eighth = iota((8, 256), 0)
    weights = []
    for h in range(2):
        column = jnp.zeros((8, 256), F32)
        for k in range(8):
            column = jnp.where(eighth == k, prior_ref[8 * h + k] * (1.0 / 16.0), column)
        weights.append(column)

    def contract(g, n):
        left, right = CHUNKS[n]
        scale = jnp.concatenate([scale_ref[:, lanes(left)], scale_ref[:, lanes(right)]], axis=1)
        for h in range(2):
            product = jnp.zeros((64, 256), F32)
            for p, lhs in ((0, lhs_re), (1, lhs_im)):
                operand = jnp.concatenate(
                    [kern_v[h, p, :, :, lanes(left)], kern_v[h, p, :, :, lanes(right)]], axis=2
                ).reshape(width, 256)
                product = product + jnp.dot(lhs[g, h, :, 0:width], operand, preferred_element_type=F32)
            factor = jnp.concatenate([weights[h] * scale] * 4, axis=0)
            for c, d in enumerate((1, 2) if g else (0, 3)):
                piece = product[32 * c : 32 * c + 32] * factor
                zpart[n, d, pl.ds(32 * h, 32), :] = piece
                zsend[n, d, pl.ds(32 * h, 32), :] = piece.astype(BF16)

    def pass_on(kind, n):
        @pl.when(middle)
        def _():
            drain(zrecv.at[n, 2 + kind], zrecv_sem.at[4 + 4 * kind + n])
            to = across if kind else far
            both = zpart[n, to] + zrecv[n, 2 + kind].astype(F32)
            zfwd[n, kind] = both.astype(BF16)
            send_along(zfwd.at[n, kind], zrecv.at[n, 1], 1 + kind, n, n, to)

    for n in range(4):
        contract(0, n)
        source, to = jnp.where(end, across, side), jnp.where(end, near, side)
        kind = jnp.where(end, 1, 0)
        send_along(zsend.at[n, source], zrecv.at[n, 2 * kind], 0, n, 4 * kind + n, to)
    drain(brecv.at[1, pl.ds(0, 7)], recv_sem.at[3])
    spread_out(1)
    for n in range(4):
        contract(1, n)

        @pl.when(end)
        def _(n=n):
            send_along(zsend.at[n, beyond], zrecv.at[n, 3], 1, n, 8 + n, near)

        if n == 1:
            pass_on(0, 0)
        if n == 2:
            pass_on(0, 1)

    def give_rest():
        for n in range(4):
            send_along(zsend.at[n, near], zrecv.at[n, 0], 2, n, n, near)

    pl.when(end)(give_rest)
    for kind, n in ((0, 2), (0, 3), (1, 0), (1, 1), (1, 2), (1, 3)):
        pass_on(kind, n)

    @pl.when(par == 0)
    def _():
        hrecv[0] = jnp.zeros((8, 128), F32)

    @pl.when(par == 3)
    def _():
        hrecv[1] = jnp.zeros((8, 128), F32)

    lane = iota((8, 128), 1)
    lane64 = iota((64, 128), 1)
    for n, (left, right) in enumerate(CHUNKS):
        drain(zrecv.at[n, pl.ds(0, 2)], zrecv_sem.at[n])
        total = zpart[n, s] + zrecv[n, 0].astype(F32) + zrecv[n, 1].astype(F32)
        zfull[:, lanes(left + 1)] = total[:, 0:128]
        zfull[:, lanes(right + 1)] = total[:, 128:256]
        if n == 0:
            for e, piece in ((0, total[:, 0:128]), (1, total[:, 128:256])):
                columns = jnp.zeros((8, 128), F32)
                for j in range(8):
                    shift = j + e
                    block = piece[8 * j : 8 * j + 8]
                    moved = block if shift == 0 else pltpu.roll(block, shift, 1)
                    columns = jnp.where(lane == j, moved, columns)
                hsend[e] = columns

            @pl.when(par > 0)
            def _():
                pltpu.make_async_remote_copy(
                    hsend.at[0], hrecv.at[1], hsend_sem.at[0], hrecv_sem.at[1],
                    device_id={"param": par - 1}, device_id_type=MESH,
                ).start()

            @pl.when(par < 3)
            def _():
                pltpu.make_async_remote_copy(
                    hsend.at[1], hrecv.at[0], hsend_sem.at[1], hrecv_sem.at[0],
                    device_id={"param": par + 1}, device_id_type=MESH,
                ).start()

        for t in READY[n]:
            if t == 0 or t == row - 1:
                e = 0 if t == 0 else 1

                @pl.when(par > 0 if e == 0 else par < 3)
                def _(e=e):
                    drain(hrecv.at[e], hrecv_sem.at[e])

                edge = hrecv[e]
                for j in range(8):
                    shift = 127 - j if e == 0 else (128 - j) % 128
                    moved = edge if shift == 0 else pltpu.roll(edge, shift, 1)
                    zfull[8 * j : 8 * j + 8, lanes(0 if e == 0 else row + 1)] = moved
            before, here, after = (zfull[:, lanes(t + i)] for i in range(3))
            low = jnp.where(lane64 == 0, pltpu.roll(before, 1, 1), pltpu.roll(here, 1, 1))
            high = jnp.where(lane64 == 127, pltpu.roll(after, 127, 1), pltpu.roll(here, 127, 1))
            smooth = (0.5 * here + 0.25 * (low + high)) * scale_ref[:, lanes(t)]
            for q in range(2):
                owner = owner_of(q, t)
                halves = [smooth[32 * h + 16 * q : 32 * h + 16 * q + 16] for h in range(2)]
                wsend[t, q] = jnp.concatenate(halves, axis=0).astype(BF16)
                piece = wsend.at[t, q]

                @pl.when(f != owner)
                def _(owner=owner, piece=piece):
                    pltpu.make_async_remote_copy(
                        piece, wrecv.at[f], send_sem.at[4], recv_sem.at[4],
                        device_id={"freq": owner}, device_id_type=MESH,
                    ).start()

                @pl.when(f == owner)
                def _(piece=piece):
                    pltpu.make_async_copy(piece, wrecv.at[f], recv_sem.at[4]).start()

    drain(wrecv, recv_sem.at[4])
    spectra = wrecv[...].reshape(512, 128)
    for half in range(2):
        rows = slice(256 * half, 256 * half + 256)
        image = jnp.dot(table_hi[rows, :], spectra, preferred_element_type=F32)
        image = image + jnp.dot(table_lo[rows, :], spectra, preferred_element_type=F32)
        isend[8 * half : 8 * half + 8] = image.astype(BF16).reshape(8, 32, 128)
        for j in (0, 1) if half == 0 else (3, 2):
            row_y = (y + 2 + j) % 4
            for i in (2, 1, 3, 0):
                if i > 0 or j != 2:
                    target_x = (x + i) % 4
                    pltpu.make_async_remote_copy(
                        isend.at[4 * j + target_x], irecv.at[slot], send_sem.at[5], recv_sem.at[5 + late],
                        device_id={"freq": 4 * row_y + target_x}, device_id_type=MESH,
                    ).start()
    pltpu.make_async_copy(isend.at[8 + x], irecv.at[slot], recv_sem.at[5 + late]).start()

    for g in range(2):
        drain(arecv.at[g, pl.ds(0, 3)], send_sem.at[g])
        drain(brecv.at[g, pl.ds(0, 7)], send_sem.at[2 + g])
    for n in range(12):
        drain(zfwd.at[0, 0], zsend_sem.at[n])

    @pl.when(par > 0)
    def _():
        drain(hsend.at[0], hsend_sem.at[0])

    @pl.when(par < 3)
    def _():
        drain(hsend.at[1], hsend_sem.at[1])

    drain(wrecv.at[pl.ds(0, 15)], send_sem.at[4])
    drain(isend.at[pl.ds(0, 15)], send_sem.at[5])
    for last in range(2):
        drain(irecv.at[pl.ds(0, 8)], recv_sem.at[5 + last])
        for q in range(2):
            for t in range(4 * last, 4 * last + 4):
                out_ref[pl.ds(2 * t + q, 26, stride=16), :] = irecv[8 * q + t, 0:26, :].astype(F32)


def local(series, kern, prior_spectrum, prior_scale):
    sensors, params = kern.shape[2:]
    series, kern = series.transpose(2, 0, 1), kern.transpose(0, 2, 1, 3)
    vmem = pltpu.VMEM
    dma = pltpu.SemaphoreType.DMA
    operands = (series, kern, prior_spectrum, prior_scale.reshape(1, -1))
    image = pl.pallas_call(
        kernel,
        out_shape=jax.ShapeDtypeStruct((416, 128), F32),
        in_specs=[
            pl.BlockSpec(memory_space=pl.ANY),
        ] * 4,
        out_specs=pl.BlockSpec(memory_space=pltpu.VMEM),
        scratch_shapes=[
            pltpu.SMEM((16,), F32),
            vmem((1, params), F32),
            vmem((26, 8, sensors), BF16),
            vmem((2, 2, sensors, 8, params), BF16),
            vmem((2, 208, 128), F32),
            vmem((2, 32, 384), F32),
            vmem((2, 4, 32, 384), BF16),
            vmem((2, 4, 32, 384), BF16),
            vmem((2, 8, 32, 384), BF16),
            vmem((2, 2, 64, 256), BF16),
            vmem((2, 2, 64, 8 * sensors), BF16),
            vmem((2, 2, 64, 8 * sensors), BF16),
            vmem((4, 4, 64, 256), BF16),
            vmem((4, 4, 64, 256), F32),
            vmem((4, 2, 64, 256), BF16),
            vmem((4, 4, 64, 256), BF16),
            vmem((64, 1280), F32),
            vmem((2, 8, 128), F32),
            vmem((2, 8, 128), F32),
            vmem((8, 2, 32, 128), BF16),
            vmem((16, 32, 128), BF16),
            vmem((16, 32, 128), BF16),
            vmem((16, 32, 128), BF16),
            vmem((512, 512), BF16),
            vmem((512, 512), BF16),
            dma((7,)),
            dma((6,)),
            dma((7,)),
            dma((12,)),
            dma((12,)),
            dma((2,)),
            dma((2,)),
        ],
        compiler_params=pltpu.CompilerParams(
            collective_id=0, has_side_effects=True, vmem_limit_bytes=50 * 1024 * 1024
        ),
        name="adjoint",
    )(*(pltpu.with_memory_space_constraint(v, pltpu.HBM) for v in operands))
    return image.reshape(26, 8, 2, 128).transpose(0, 2, 1, 3).reshape(26, 2, params)


def solution(mesh):
    placed = (P(None, "sens", "freq"), P(None, "freq", "sens", "param"), P("freq"), P("param"))
    return jax.shard_map(
        local, mesh=mesh, in_specs=placed, out_specs=P("freq", "sens", "param"), check_vma=False
    )
```

time: 45.2 us -> 41 us (0.907)
  the two profiles are of different devices: /device:TPU:32 before, /device:TPU:1 now
where the time goes in v2:
time: 41 us; the launch traced here: 40.9 us
  Pallas kernels  40.2 us (98%)
  local copies, waits for them, and re-layouts  0.69 us (2%)
    pallas_call x1, Pallas kernels, local(): pl.pallas_call(kernel, out_shape=jax.ShapeDtypeStruct((416, 128), F32), i...  40.2 us

profile of v2, /device:TPU:1, one launch (start us, length us, event | category | flops | bytes accessed | tf_op | source)
XLA Modules:
  0.0 40.9 jit_solution(17005084634511390020)
XLA Ops:
  0.0 40.2 %adjoint.1 = f32[416,128]{1,0:T(8,128)S(1)} custom-call(bf16[26,8,150]{2,1,0:T(8,128)(2,1)} %bitcast.10, bf16[2,150,16,1024]{3,2,1,0:T(8,128)(2,1)} %bitcast.9, f32[16]{0:T(128)} %prior_hbm.1, f32[1,1024]{1,0:T(1,128)} %bitcast.11), custom_call_target="tpu_custom_call" | custom-call | tf_op jit(solution)/shard_map/adjoint/pallas_call | solution.py:389
  40.2 0.7 %copy.7 = f32[26,2,1024]{2,1,0:T(2,128)} copy(f32[26,2,1024]{2,1,0:T(2,128)S(1)} %bitcast.8) | data formatting | bytes 425984

commit v3 on v2

--- a/solution.py
+++ b/solution.py
@@ -12,7 +12,7 @@
 MESH = pl.DeviceIdType.MESH
 F32, BF16 = jnp.float32, jnp.bfloat16
 CHUNKS = ((0, 7), (1, 2), (3, 4), (5, 6))
-READY = ((), (0, 1), (2, 3), (4, 5, 6, 7))
+READY = ((), (1,), (2, 3, 0), (4, 5, 6, 7))
 STEPS = sorted(((i, j) for i in range(4) for j in range(4) if i + j), key=lambda v: -sum(min(a, 4 - a) for a in v))
 
 
@@ -47,7 +47,7 @@
     series_ref, kern_ref, prior_hbm, scale_hbm, out_ref,
     prior_ref, scale_ref, ser_v, kern_v, by_time, turned, arecv, bsend, brecv, packed, lhs_re, lhs_im, zsend, zpart, zfwd, zrecv, zfull,
     hsend, hrecv, wsend, wrecv, isend, irecv, table_hi, table_lo,
-    local_sem, send_sem, recv_sem, zsend_sem, zrecv_sem, hsend_sem, hrecv_sem,
+    local_sem, send_sem, recv_sem, zsend_sem, zrecv_sem, hsend_sem, hrecv_sem, round_sem,
 ):
     f, par, s = lax.axis_index("freq"), lax.axis_index("param"), lax.axis_index("sens")
     y, x = f // 4, f % 4
@@ -69,23 +69,23 @@
     second_pos = y * (1 - core) + x * core
 
     barrier = pltpu.get_barrier_semaphore()
-    for i, j in sorted(STEPS, key=sum):
-        peer = 4 * ((y + j) % 4) + (x + i) % 4
-        pl.semaphore_signal(barrier, 1, device_id={"freq": peer}, device_id_type=MESH)
+    other = par + 1 - 2 * core
+    in_plane = [{"freq": first_at((first_pos + o) % 4)} for o in (2, 1, 3)] + [{"param": other}]
+
+    def greet(sem, peers):
+        for peer in peers:
+            pl.semaphore_signal(sem, 1, device_id=peer, device_id_type=MESH)
+
+    greet(barrier, in_plane)
     for o in range(1, 4):
-        pl.semaphore_signal(barrier, 1, device_id={"sens": (s + o) % 4}, device_id_type=MESH)
-    other = par + 1 - 2 * core
-    for m in range(4):
-        source = m * (1 + 3 * core) + 4 * y * (1 - core) + x * core
-        pl.semaphore_signal(barrier, 1, device_id={"freq": source, "param": other}, device_id_type=MESH)
+
+        @pl.when(s + o < 4)
+        def _(o=o):
+            greet(barrier, [{"sens": s + o}, {"sens": s + o, "param": other}])
 
     @pl.when(par == 1)
     def _():
-        pl.semaphore_signal(barrier, 1, device_id={"param": 2}, device_id_type=MESH)
-
-    @pl.when(par == 2)
-    def _():
-        pl.semaphore_signal(barrier, 1, device_id={"param": 1}, device_id_type=MESH)
+        greet(barrier, [{"sens": d, "param": 2} for d in range(4)])
 
     series_in = pltpu.make_async_copy(series_ref, ser_v, local_sem.at[0])
     series_in.start()
@@ -122,7 +122,7 @@
             turned[g, 0:26, 256 + 32 * q : 256 + 32 * q + rest_of] = by_time[1, rows, :][:, 0:rest_of]
         arecv[g, first_pos] = turned[g].astype(BF16)
 
-    pl.semaphore_wait(barrier, 22 + jnp.where((par == 1) | (par == 2), 1, 0))
+    pl.semaphore_wait(barrier, 4 + 2 * s + jnp.where(par == 2, 4, 0))
 
     for g in range(2):
         for o in (2, 1, 3):
@@ -130,6 +130,19 @@
                 arecv.at[g, first_pos], arecv.at[g, first_pos], send_sem.at[g], recv_sem.at[g],
                 device_id={"freq": first_at((first_pos + o) % 4)}, device_id_type=MESH,
             ).start()
+
+    greet(round_sem.at[0], in_plane)
+
+    for o in range(1, 4):
+
+        @pl.when(s >= o)
+        def _(o=o):
+            greet(round_sem.at[2], [{"sens": s - o}])
+            greet(round_sem.at[3], [{"sens": s - o, "param": other}])
+
+    @pl.when(par == 2)
+    def _():
+        greet(round_sem.at[3], [{"sens": d, "param": 1} for d in range(4)])
 
     @pl.loop(0, 16)
     def _(b):
@@ -144,6 +157,8 @@
     def drain(like, sem):
         pltpu.make_async_copy(like, like, sem).wait()
 
+    pl.semaphore_wait(round_sem.at[0], 4)
+    greet(round_sem.at[1], in_plane)
     for g in range(2):
         drain(arecv.at[g, pl.ds(0, 3)], recv_sem.at[g])
         gathered = arecv[g].reshape(128, 384)
@@ -151,6 +166,8 @@
         spec = spec + jnp.dot(fwd_lo, gathered, preferred_element_type=F32)
         spec = spec * (1.0 / math.sqrt(416.0))
         bsend[g] = spec.astype(BF16).reshape(4, 32, 384)
+        if g == 0:
+            pl.semaphore_wait(round_sem.at[1], 4)
         for o in (2, 1, 3, 0):
             m = (second_pos + o) % 4
             for c in range(2):
@@ -197,6 +214,11 @@
     for copy in small_in + kernel_in:
         copy.wait()
 
+    @pl.when(s < 3)
+    def _():
+        pl.semaphore_wait(round_sem.at[2], 3 - s)
+
+
     def send_along(source, target, kind, n, received, to):
         pltpu.make_async_remote_copy(
             source, target, zsend_sem.at[4 * kind + n], zrecv_sem.at[received],
@@ -213,6 +235,11 @@
         for k in range(8):
             column = jnp.where(eighth == k, prior_ref[8 * h + k] * (1.0 / 16.0), column)
         weights.append(column)
+
+    def lead(n):
+        source, to = jnp.where(end, across, side), jnp.where(end, near, side)
+        kind = jnp.where(end, 1, 0)
+        send_along(zsend.at[n, source], zrecv.at[n, 2 * kind], 0, n, 4 * kind + n, to)
 
     def contract(g, n):
         left, right = CHUNKS[n]
@@ -239,11 +266,45 @@
             zfwd[n, kind] = both.astype(BF16)
             send_along(zfwd.at[n, kind], zrecv.at[n, 1], 1 + kind, n, n, to)
 
+    lane8 = iota((8, 128), 1)
+
+    @pl.when(par == 0)
+    def _():
+        hrecv[0] = jnp.zeros((4, 8, 128), BF16)
+
+    @pl.when(par == 3)
+    def _():
+        hrecv[1] = jnp.zeros((4, 8, 128), BF16)
+
+    def send_edges(g):
+        for d in (1, 2) if g else (0, 3):
+            for e in range(2):
+                columns = jnp.zeros((8, 128), F32)
+                for j in range(8):
+                    block = zpart[0, d, 8 * j : 8 * j + 8, lanes(e)]
+                    moved = block if j + e == 0 else pltpu.roll(block, j + e, 1)
+                    columns = jnp.where(lane8 == j, moved, columns)
+                hsend[e, d] = columns.astype(BF16)
+
+        @pl.when(par > 0)
+        def _():
+            for d in (1, 2) if g else (0, 3):
+                pltpu.make_async_remote_copy(
+                    hsend.at[0, d], hrecv.at[1, s], hsend_sem.at[0], hrecv_sem.at[1],
+                    device_id={"param": par - 1, "sens": d}, device_id_type=MESH,
+                ).start()
+
+        @pl.when(par < 3)
+        def _():
+            for d in (1, 2) if g else (0, 3):
+                pltpu.make_async_remote_copy(
+                    hsend.at[1, d], hrecv.at[0, s], hsend_sem.at[1], hrecv_sem.at[0],
+                    device_id={"param": par + 1, "sens": d}, device_id_type=MESH,
+                ).start()
+
     for n in range(4):
         contract(0, n)
-        source, to = jnp.where(end, across, side), jnp.where(end, near, side)
-        kind = jnp.where(end, 1, 0)
-        send_along(zsend.at[n, source], zrecv.at[n, 2 * kind], 0, n, 4 * kind + n, to)
+        lead(n)
     drain(brecv.at[1, pl.ds(0, 7)], recv_sem.at[3])
     spread_out(1)
     for n in range(4):
@@ -253,6 +314,14 @@
         def _(n=n):
             send_along(zsend.at[n, beyond], zrecv.at[n, 3], 1, n, 8 + n, near)
 
+        if n == 0:
+
+            @pl.when((s < 3) | (par == 1))
+            def _():
+                pl.semaphore_wait(round_sem.at[3], 3 - s + jnp.where(par == 1, 4, 0))
+
+            send_edges(0)
+            send_edges(1)
         if n == 1:
             pass_on(0, 0)
         if n == 2:
@@ -266,45 +335,12 @@
     for kind, n in ((0, 2), (0, 3), (1, 0), (1, 1), (1, 2), (1, 3)):
         pass_on(kind, n)
 
-    @pl.when(par == 0)
-    def _():
-        hrecv[0] = jnp.zeros((8, 128), F32)
-
-    @pl.when(par == 3)
-    def _():
-        hrecv[1] = jnp.zeros((8, 128), F32)
-
-    lane = iota((8, 128), 1)
     lane64 = iota((64, 128), 1)
     for n, (left, right) in enumerate(CHUNKS):
         drain(zrecv.at[n, pl.ds(0, 2)], zrecv_sem.at[n])
         total = zpart[n, s] + zrecv[n, 0].astype(F32) + zrecv[n, 1].astype(F32)
         zfull[:, lanes(left + 1)] = total[:, 0:128]
         zfull[:, lanes(right + 1)] = total[:, 128:256]
-        if n == 0:
-            for e, piece in ((0, total[:, 0:128]), (1, total[:, 128:256])):
-                columns = jnp.zeros((8, 128), F32)
-                for j in range(8):
-                    shift = j + e
-                    block = piece[8 * j : 8 * j + 8]
-                    moved = block if shift == 0 else pltpu.roll(block, shift, 1)
-                    columns = jnp.where(lane == j, moved, columns)
-                hsend[e] = columns
-
-            @pl.when(par > 0)
-            def _():
-                pltpu.make_async_remote_copy(
-                    hsend.at[0], hrecv.at[1], hsend_sem.at[0], hrecv_sem.at[1],
-                    device_id={"param": par - 1}, device_id_type=MESH,
-                ).start()
-
-            @pl.when(par < 3)
-            def _():
-                pltpu.make_async_remote_copy(
-                    hsend.at[1], hrecv.at[0], hsend_sem.at[1], hrecv_sem.at[0],
-                    device_id={"param": par + 1}, device_id_type=MESH,
-                ).start()
-
         for t in READY[n]:
             if t == 0 or t == row - 1:
                 e = 0 if t == 0 else 1
@@ -313,7 +349,9 @@
                 def _(e=e):
                     drain(hrecv.at[e], hrecv_sem.at[e])
 
-                edge = hrecv[e]
+                edge = hrecv[e, 0].astype(F32)
+                for o in range(1, 4):
+                    edge = edge + hrecv[e, o].astype(F32)
                 for j in range(8):
                     shift = 127 - j if e == 0 else (128 - j) % 128
                     moved = edge if shift == 0 else pltpu.roll(edge, shift, 1)
@@ -411,8 +449,8 @@
             vmem((4, 2, 64, 256), BF16),
             vmem((4, 4, 64, 256), BF16),
             vmem((64, 1280), F32),
-            vmem((2, 8, 128), F32),
-            vmem((2, 8, 128), F32),
+            vmem((2, 4, 8, 128), BF16),
+            vmem((2, 4, 8, 128), BF16),
             vmem((8, 2, 32, 128), BF16),
             vmem((16, 32, 128), BF16),
             vmem((16, 32, 128), BF16),
@@ -426,6 +464,7 @@
             dma((12,)),
             dma((2,)),
             dma((2,)),
+            pltpu.SemaphoreType.REGULAR((4,)),
         ],
         compiler_params=pltpu.CompilerParams(
             collective_id=0, has_side_effects=True, vmem_limit_bytes=50 * 1024 * 1024

time: 41 us -> 37 us (0.902)
  the two profiles are of different devices: /device:TPU:1 before, /device:TPU:32 now
where the time goes in v3:
time: 37 us
  Pallas kernels  36.3 us (98%)
  local copies, waits for them, and re-layouts  0.69 us (2%)
    pallas_call x1, Pallas kernels, local(): pl.pallas_call(kernel, out_shape=jax.ShapeDtypeStruct((416, 128), F32), i...  36.3 us

profile of v3, /device:TPU:32, one launch (start us, length us, event | category | flops | bytes accessed | tf_op | source)
XLA Modules:
  0.0 37.0 jit_solution(14801247845516853496)
XLA Ops:
  0.0 36.3 %adjoint.1 = f32[416,128]{1,0:T(8,128)S(1)} custom-call(bf16[26,8,150]{2,1,0:T(8,128)(2,1)} %bitcast.10, bf16[2,150,16,1024]{3,2,1,0:T(8,128)(2,1)} %bitcast.9, f32[16]{0:T(128)} %prior_hbm.1, f32[1,1024]{1,0:T(1,128)} %bitcast.11), custom_call_target="tpu_custom_call" | custom-call | tf_op jit(solution)/shard_map/adjoint/pallas_call | solution.py:427
  36.3 0.7 %copy.7 = f32[26,2,1024]{2,1,0:T(2,128)} copy(f32[26,2,1024]{2,1,0:T(2,128)S(1)} %bitcast.8) | data formatting | bytes 425984

commit v4 on v3

--- a/solution.py
+++ b/solution.py
@@ -12,14 +12,8 @@
 MESH = pl.DeviceIdType.MESH
 F32, BF16 = jnp.float32, jnp.bfloat16
 CHUNKS = ((0, 7), (1, 2), (3, 4), (5, 6))
-READY = ((), (1,), (2, 3, 0), (4, 5, 6, 7))
+READY = ((), (), (0, 1, 2, 3), (4, 5, 6, 7))
 STEPS = sorted(((i, j) for i in range(4) for j in range(4) if i + j), key=lambda v: -sum(min(a, 4 - a) for a in v))
-
-
-def owner_of(half, tile):
-    early, low = int(tile < 4), tile % 4
-    at_y = 2 * half + low // 2
-    return 4 * at_y + 2 * (low % 2) + (early + at_y) % 2
 
 
 def iota(shape, dim):
@@ -46,7 +40,7 @@
 def kernel(
     series_ref, kern_ref, prior_hbm, scale_hbm, out_ref,
     prior_ref, scale_ref, ser_v, kern_v, by_time, turned, arecv, bsend, brecv, packed, lhs_re, lhs_im, zsend, zpart, zfwd, zrecv, zfull,
-    hsend, hrecv, wsend, wrecv, isend, irecv, table_hi, table_lo,
+    hsend, hrecv, wsend, wrecv, isend, irecv, out_v, table_hi, table_lo,
     local_sem, send_sem, recv_sem, zsend_sem, zrecv_sem, hsend_sem, hrecv_sem, round_sem,
 ):
     f, par, s = lax.axis_index("freq"), lax.axis_index("param"), lax.axis_index("sens")
@@ -68,6 +62,8 @@
     first_pos = x * (1 - core) + y * core
     second_pos = y * (1 - core) + x * core
 
+    series_in = pltpu.make_async_copy(series_ref, ser_v, local_sem.at[0])
+    series_in.start()
     barrier = pltpu.get_barrier_semaphore()
     other = par + 1 - 2 * core
     in_plane = [{"freq": first_at((first_pos + o) % 4)} for o in (2, 1, 3)] + [{"param": other}]
@@ -87,8 +83,6 @@
     def _():
         greet(barrier, [{"sens": d, "param": 2} for d in range(4)])
 
-    series_in = pltpu.make_async_copy(series_ref, ser_v, local_sem.at[0])
-    series_in.start()
     small_in = []
     for n, (source, target) in enumerate(((prior_hbm, prior_ref), (scale_hbm, scale_ref))):
         small_in.append(pltpu.make_async_copy(source, target, local_sem.at[5 + n]))
@@ -257,14 +251,18 @@
                 zpart[n, d, pl.ds(32 * h, 32), :] = piece
                 zsend[n, d, pl.ds(32 * h, 32), :] = piece.astype(BF16)
 
+    def parts_of(kind, n):
+        return (pl.ds(0, 32), pl.ds(32, 32)) if kind == 1 and n == 3 else (pl.ds(0, 64),)
+
     def pass_on(kind, n):
         @pl.when(middle)
         def _():
-            drain(zrecv.at[n, 2 + kind], zrecv_sem.at[4 + 4 * kind + n])
             to = across if kind else far
-            both = zpart[n, to] + zrecv[n, 2 + kind].astype(F32)
-            zfwd[n, kind] = both.astype(BF16)
-            send_along(zfwd.at[n, kind], zrecv.at[n, 1], 1 + kind, n, n, to)
+            for m, part in enumerate(parts_of(kind, n)):
+                drain(zrecv.at[n, 2 + kind, part], zrecv_sem.at[12 if m else 4 + 4 * kind + n])
+                both = zpart[n, to, part] + zrecv[n, 2 + kind, part].astype(F32)
+                zfwd[n, kind, part] = both.astype(BF16)
+                send_along(zfwd.at[n, kind, part], zrecv.at[n, 1, part], 1 + kind, n, n, to)
 
     lane8 = iota((8, 128), 1)
 
@@ -312,7 +310,8 @@
 
         @pl.when(end)
         def _(n=n):
-            send_along(zsend.at[n, beyond], zrecv.at[n, 3], 1, n, 8 + n, near)
+            for m, part in enumerate(parts_of(1, n)):
+                send_along(zsend.at[n, beyond, part], zrecv.at[n, 3, part], 1, n, 12 if m else 8 + n, near)
 
         if n == 0:
 
@@ -341,9 +340,8 @@
         total = zpart[n, s] + zrecv[n, 0].astype(F32) + zrecv[n, 1].astype(F32)
         zfull[:, lanes(left + 1)] = total[:, 0:128]
         zfull[:, lanes(right + 1)] = total[:, 128:256]
-        for t in READY[n]:
-            if t == 0 or t == row - 1:
-                e = 0 if t == 0 else 1
+        for e, t in ((0, 0), (1, row - 1)):
+            if t in READY[n]:
 
                 @pl.when(par > 0 if e == 0 else par < 3)
                 def _(e=e):
@@ -356,26 +354,31 @@
                     shift = 127 - j if e == 0 else (128 - j) % 128
                     moved = edge if shift == 0 else pltpu.roll(edge, shift, 1)
                     zfull[8 * j : 8 * j + 8, lanes(0 if e == 0 else row + 1)] = moved
+        for t in READY[n]:
             before, here, after = (zfull[:, lanes(t + i)] for i in range(3))
             low = jnp.where(lane64 == 0, pltpu.roll(before, 1, 1), pltpu.roll(here, 1, 1))
             high = jnp.where(lane64 == 127, pltpu.roll(after, 127, 1), pltpu.roll(here, 127, 1))
             smooth = (0.5 * here + 0.25 * (low + high)) * scale_ref[:, lanes(t)]
             for q in range(2):
-                owner = owner_of(q, t)
                 halves = [smooth[32 * h + 16 * q : 32 * h + 16 * q + 16] for h in range(2)]
                 wsend[t, q] = jnp.concatenate(halves, axis=0).astype(BF16)
-                piece = wsend.at[t, q]
-
-                @pl.when(f != owner)
-                def _(owner=owner, piece=piece):
-                    pltpu.make_async_remote_copy(
-                        piece, wrecv.at[f], send_sem.at[4], recv_sem.at[4],
-                        device_id={"freq": owner}, device_id_type=MESH,
-                    ).start()
-
-                @pl.when(f == owner)
-                def _(piece=piece):
-                    pltpu.make_async_copy(piece, wrecv.at[f], recv_sem.at[4]).start()
+        if n >= 2:
+            upper = n - 2
+            for mine in range(2):
+
+                @pl.when(late == mine)
+                def _(upper=upper, mine=mine):
+                    for i, j in STEPS:
+                        if (i + j + mine + upper) % 2 == 0:
+                            to_y, to_x = (y + j) % 4, (x + i) % 4
+                            t = 4 * upper + 2 * (to_y % 2) + to_x // 2
+                            pltpu.make_async_remote_copy(
+                                wsend.at[t, to_y // 2], wrecv.at[f], send_sem.at[4], recv_sem.at[4],
+                                device_id={"freq": 4 * to_y + to_x}, device_id_type=MESH,
+                            ).start()
+                    if mine == upper:
+                        own = wsend.at[4 * upper + 2 * (y % 2) + x // 2, y // 2]
+                        pltpu.make_async_copy(own, wrecv.at[f], recv_sem.at[4]).start()
 
     drain(wrecv, recv_sem.at[4])
     spectra = wrecv[...].reshape(512, 128)
@@ -411,11 +414,21 @@
 
     drain(wrecv.at[pl.ds(0, 15)], send_sem.at[4])
     drain(isend.at[pl.ds(0, 15)], send_sem.at[5])
+    out_copies = []
     for last in range(2):
         drain(irecv.at[pl.ds(0, 8)], recv_sem.at[5 + last])
         for q in range(2):
-            for t in range(4 * last, 4 * last + 4):
-                out_ref[pl.ds(2 * t + q, 26, stride=16), :] = irecv[8 * q + t, 0:26, :].astype(F32)
+            for t in range(4):
+                piece = irecv[8 * q + 4 * last + t, 0:26, :].astype(F32)
+                out_v[last, pl.ds(2 * t + q, 26, stride=8), :] = piece
+        out_copies.append(
+            pltpu.make_async_copy(
+                out_v.at[last].reshape(26, 8, 128), out_ref.at[:, pl.ds(8 * last, 8)], local_sem.at[last]
+            )
+        )
+        out_copies[-1].start()
+    for copy in out_copies:
+        copy.wait()
 
 
 def local(series, kern, prior_spectrum, prior_scale):
@@ -426,11 +439,11 @@
     operands = (series, kern, prior_spectrum, prior_scale.reshape(1, -1))
     image = pl.pallas_call(
         kernel,
-        out_shape=jax.ShapeDtypeStruct((416, 128), F32),
+        out_shape=jax.ShapeDtypeStruct((26, 16, 128), F32),
         in_specs=[
             pl.BlockSpec(memory_space=pl.ANY),
         ] * 4,
-        out_specs=pl.BlockSpec(memory_space=pltpu.VMEM),
+        out_specs=pl.BlockSpec(memory_space=pl.ANY),
         scratch_shapes=[
             pltpu.SMEM((16,), F32),
             vmem((1, params), F32),
@@ -455,13 +468,14 @@
             vmem((16, 32, 128), BF16),
             vmem((16, 32, 128), BF16),
             vmem((16, 32, 128), BF16),
+            vmem((2, 208, 128), F32),
             vmem((512, 512), BF16),
             vmem((512, 512), BF16),
             dma((7,)),
             dma((6,)),
             dma((7,)),
             dma((12,)),
-            dma((12,)),
+            dma((13,)),
             dma((2,)),
             dma((2,)),
             pltpu.SemaphoreType.REGULAR((4,)),

time: 37 us -> 36.8 us (level)
  no operation moved by 1% of the time
where the time goes in v4:
time: 36.8 us; the launch traced here: 36.7 us
  Pallas kernels  36 us (98%)
  local copies, waits for them, and re-layouts  0.69 us (2%)
    pallas_call x1, Pallas kernels, local(): pl.pallas_call(kernel, out_shape=jax.ShapeDtypeStruct((26, 16, 128), F32)...  36 us

profile of v4, /device:TPU:32, one launch (start us, length us, event | category | flops | bytes accessed | tf_op | source)
XLA Modules:
  0.0 36.7 jit_solution(10488274883475273328)
XLA Ops:
  0.0 36.0 %adjoint.1 = f32[26,16,128]{2,1,0:T(8,128)S(1)} custom-call(bf16[26,8,150]{2,1,0:T(8,128)(2,1)} %bitcast.10, bf16[2,150,16,1024]{3,2,1,0:T(8,128)(2,1)} %bitcast.9, f32[16]{0:T(128)} %prior_hbm.1, f32[1,1024]{1,0:T(1,128)} %bitcast.11), custom_call_target="tpu_custom_call" | custom-call | tf_op jit(solution)/shard_map/adjoint/pallas_call | solution.py:440
  36.0 0.7 %copy.7 = f32[26,2,1024]{2,1,0:T(2,128)} copy(f32[26,2,1024]{2,1,0:T(2,128)S(1)} %bitcast.8) | data formatting | bytes 425984

commit v5 on v4

--- a/solution.py
+++ b/solution.py
@@ -107,8 +107,8 @@
     turned[:, 24:32, :] = jnp.zeros((2, 8, 384), F32)
     turned[:, :, 256:384] = jnp.zeros((2, 32, 128), F32)
     series_in.wait()
-    by_time[0] = ser_v[:, :, 0:128].astype(F32).reshape(208, 128)
-    by_time[1, :, 0:rest_of] = ser_v[:, :, 128:sensors].astype(F32).reshape(208, rest_of)
+    by_time[0, 0:208, :] = ser_v[:, :, 0:128].astype(F32).reshape(208, 128)
+    by_time[1, 0:208, 0:rest_of] = ser_v[:, :, 128:sensors].astype(F32).reshape(208, rest_of)
     for g in range(2):
         for q in range(2):
             rows = pl.ds((6 * core if g == 0 else 2 + 2 * core) + q, 26, stride=8)
@@ -423,7 +423,7 @@
                 out_v[last, pl.ds(2 * t + q, 26, stride=8), :] = piece
         out_copies.append(
             pltpu.make_async_copy(
-                out_v.at[last].reshape(26, 8, 128), out_ref.at[:, pl.ds(8 * last, 8)], local_sem.at[last]
+                out_v.at[last, pl.ds(0, 208)].reshape(26, 8, 128), out_ref.at[:, pl.ds(8 * last, 8)], local_sem.at[last]
             )
         )
         out_copies[-1].start()
@@ -449,14 +449,14 @@
             vmem((1, params), F32),
             vmem((26, 8, sensors), BF16),
             vmem((2, 2, sensors, 8, params), BF16),
-            vmem((2, 208, 128), F32),
+            vmem((2, 256, 128), F32),
             vmem((2, 32, 384), F32),
             vmem((2, 4, 32, 384), BF16),
             vmem((2, 4, 32, 384), BF16),
             vmem((2, 8, 32, 384), BF16),
             vmem((2, 2, 64, 256), BF16),
-            vmem((2, 2, 64, 8 * sensors), BF16),
-            vmem((2, 2, 64, 8 * sensors), BF16),
+            vmem((2, 2, 64, 256 * pl.cdiv(8 * sensors, 256)), BF16),
+            vmem((2, 2, 64, 256 * pl.cdiv(8 * sensors, 256)), BF16),
             vmem((4, 4, 64, 256), BF16),
             vmem((4, 4, 64, 256), F32),
             vmem((4, 2, 64, 256), BF16),
@@ -468,7 +468,7 @@
             vmem((16, 32, 128), BF16),
             vmem((16, 32, 128), BF16),
             vmem((16, 32, 128), BF16),
-            vmem((2, 208, 128), F32),
+            vmem((2, 256, 128), F32),
             vmem((512, 512), BF16),
             vmem((512, 512), BF16),
             dma((7,)),

time: 36.8 us -> 36.8 us (level)
  no operation moved by 1% of the time
where the time goes in v5:
time: 36.8 us; the launch traced here: 36.7 us
  Pallas kernels  36 us (98%)
  local copies, waits for them, and re-layouts  0.69 us (2%)
    pallas_call x1, Pallas kernels, local(): pl.pallas_call(kernel, out_shape=jax.ShapeDtypeStruct((26, 16, 128), F32)...  36 us

profile of v5, /device:TPU:32, one launch (start us, length us, event | category | flops | bytes accessed | tf_op | source)
XLA Modules:
  0.0 36.7 jit_solution(5954862818605799745)
XLA Ops:
  0.0 36.0 %adjoint.1 = f32[26,16,128]{2,1,0:T(8,128)S(1)} custom-call(bf16[26,8,150]{2,1,0:T(8,128)(2,1)} %bitcast.10, bf16[2,150,16,1024]{3,2,1,0:T(8,128)(2,1)} %bitcast.9, f32[16]{0:T(128)} %prior_hbm.1, f32[1,1024]{1,0:T(1,128)} %bitcast.11), custom_call_target="tpu_custom_call" | custom-call | tf_op jit(solution)/shard_map/adjoint/pallas_call | solution.py:440
  36.0 0.7 %copy.7 = f32[26,2,1024]{2,1,0:T(2,128)} copy(f32[26,2,1024]{2,1,0:T(2,128)S(1)} %bitcast.8) | data formatting | bytes 425984

commit v6 on v5

--- a/solution.py
+++ b/solution.py
@@ -40,7 +40,7 @@
 def kernel(
     series_ref, kern_ref, prior_hbm, scale_hbm, out_ref,
     prior_ref, scale_ref, ser_v, kern_v, by_time, turned, arecv, bsend, brecv, packed, lhs_re, lhs_im, zsend, zpart, zfwd, zrecv, zfull,
-    hsend, hrecv, wsend, wrecv, isend, irecv, out_v, table_hi, table_lo,
+    hsend, hrecv, wsend, wrecv, isend, irecv, out_v, spreads, table_hi, table_lo,
     local_sem, send_sem, recv_sem, zsend_sem, zrecv_sem, hsend_sem, hrecv_sem, round_sem,
 ):
     f, par, s = lax.axis_index("freq"), lax.axis_index("param"), lax.axis_index("sens")
@@ -150,6 +150,11 @@
 
     def drain(like, sem):
         pltpu.make_async_copy(like, like, sem).wait()
+
+    for at in range(0, 8 * sensors, 256):
+        size = min(256, 8 * sensors - at)
+        spread = (iota((sensors, size), 0) == (at + iota((sensors, size), 1)) // 8).astype(BF16)
+        spreads[0:sensors, at : at + size] = spread
 
     pl.semaphore_wait(round_sem.at[0], 4)
     greet(round_sem.at[1], in_plane)
@@ -194,8 +199,7 @@
         compact = packed[g].reshape(128, 256)[:, 0:sensors]
         for at in range(0, width, 256):
             size = min(256, width - at)
-            spread = (iota((sensors, size), 0) == (at + iota((sensors, size), 1)) // 8).astype(BF16)
-            spaced = jnp.dot(compact, spread, preferred_element_type=F32)
+            spaced = jnp.dot(compact, spreads[0:sensors, at : at + size], preferred_element_type=F32)
             for r in range(8):
                 block = jnp.where(diagonal[:, 0:size], spaced[16 * r : 16 * r + 16], 0.0)
                 rows = slice(16 * (r % 4), 16 * (r % 4) + 16)
@@ -252,14 +256,14 @@
                 zsend[n, d, pl.ds(32 * h, 32), :] = piece.astype(BF16)
 
     def parts_of(kind, n):
-        return (pl.ds(0, 32), pl.ds(32, 32)) if kind == 1 and n == 3 else (pl.ds(0, 64),)
+        return [pl.ds(16 * m, 16) for m in range(4)] if kind == 1 and n == 3 else [pl.ds(0, 64)]
 
     def pass_on(kind, n):
         @pl.when(middle)
         def _():
             to = across if kind else far
             for m, part in enumerate(parts_of(kind, n)):
-                drain(zrecv.at[n, 2 + kind, part], zrecv_sem.at[12 if m else 4 + 4 * kind + n])
+                drain(zrecv.at[n, 2 + kind, part], zrecv_sem.at[11 + m if m else 4 + 4 * kind + n])
                 both = zpart[n, to, part] + zrecv[n, 2 + kind, part].astype(F32)
                 zfwd[n, kind, part] = both.astype(BF16)
                 send_along(zfwd.at[n, kind, part], zrecv.at[n, 1, part], 1 + kind, n, n, to)
@@ -311,7 +315,7 @@
         @pl.when(end)
         def _(n=n):
             for m, part in enumerate(parts_of(1, n)):
-                send_along(zsend.at[n, beyond, part], zrecv.at[n, 3, part], 1, n, 12 if m else 8 + n, near)
+                send_along(zsend.at[n, beyond, part], zrecv.at[n, 3, part], 1, n, 11 + m if m else 8 + n, near)
 
         if n == 0:
 
@@ -469,13 +473,14 @@
             vmem((16, 32, 128), BF16),
             vmem((16, 32, 128), BF16),
             vmem((2, 256, 128), F32),
+            vmem((pl.cdiv(sensors, 16) * 16, 256 * pl.cdiv(8 * sensors, 256)), BF16),
             vmem((512, 512), BF16),
             vmem((512, 512), BF16),
             dma((7,)),
             dma((6,)),
             dma((7,)),
             dma((12,)),
-            dma((13,)),
+            dma((15,)),
             dma((2,)),
             dma((2,)),
             pltpu.SemaphoreType.REGULAR((4,)),

time: 36.8 us -> 36.8 us (level)
  no operation moved by 1% of the time
where the time goes in v6:
time: 36.8 us; the launch traced here: 36.7 us
  Pallas kernels  36 us (98%)
  local copies, waits for them, and re-layouts  0.69 us (2%)
    pallas_call x1, Pallas kernels, local(): pl.pallas_call(kernel, out_shape=jax.ShapeDtypeStruct((26, 16, 128), F32)...  36 us

profile of v6, /device:TPU:32, one launch (start us, length us, event | category | flops | bytes accessed | tf_op | source)
XLA Modules:
  0.0 36.7 jit_solution(12118905994255832286)
XLA Ops:
  0.0 36.0 %adjoint.1 = f32[26,16,128]{2,1,0:T(8,128)S(1)} custom-call(bf16[26,8,150]{2,1,0:T(8,128)(2,1)} %bitcast.10, bf16[2,150,16,1024]{3,2,1,0:T(8,128)(2,1)} %bitcast.9, f32[16]{0:T(128)} %prior_hbm.1, f32[1,1024]{1,0:T(1,128)} %bitcast.11), custom_call_target="tpu_custom_call" | custom-call | tf_op jit(solution)/shard_map/adjoint/pallas_call | solution.py:444
  36.0 0.7 %copy.7 = f32[26,2,1024]{2,1,0:T(2,128)} copy(f32[26,2,1024]{2,1,0:T(2,128)S(1)} %bitcast.8) | data formatting | bytes 425984

commit v7 on v5

--- a/solution.py
+++ b/solution.py
@@ -62,8 +62,6 @@
     first_pos = x * (1 - core) + y * core
     second_pos = y * (1 - core) + x * core
 
-    series_in = pltpu.make_async_copy(series_ref, ser_v, local_sem.at[0])
-    series_in.start()
     barrier = pltpu.get_barrier_semaphore()
     other = par + 1 - 2 * core
     in_plane = [{"freq": first_at((first_pos + o) % 4)} for o in (2, 1, 3)] + [{"param": other}]
@@ -73,6 +71,8 @@
             pl.semaphore_signal(sem, 1, device_id=peer, device_id_type=MESH)
 
     greet(barrier, in_plane)
+    series_in = pltpu.make_async_copy(series_ref, ser_v, local_sem.at[0])
+    series_in.start()
     for o in range(1, 4):
 
         @pl.when(s + o < 4)
@@ -95,7 +95,6 @@
                     kern_ref.at[p, :, pl.ds(8 * h, 8)], kern_v.at[h, p], local_sem.at[1 + 2 * h + p]
                 )
             )
-            kernel_in[-1].start()
 
     ri, ci = iota((128, 128), 0), iota((128, 128), 1)
     bins = 16 * second_at(ri >> 5) + (ri & 15)
@@ -107,6 +106,8 @@
     turned[:, 24:32, :] = jnp.zeros((2, 8, 384), F32)
     turned[:, :, 256:384] = jnp.zeros((2, 32, 128), F32)
     series_in.wait()
+    for copy in kernel_in:
+        copy.start()
     by_time[0, 0:208, :] = ser_v[:, :, 0:128].astype(F32).reshape(208, 128)
     by_time[1, 0:208, 0:rest_of] = ser_v[:, :, 128:sensors].astype(F32).reshape(208, rest_of)
     for g in range(2):

time: 36.8 us -> 36.8 us (level)
  no operation moved by 1% of the time
where the time goes in v7:
time: 36.8 us; the launch traced here: 36.7 us
  Pallas kernels  36 us (98%)
  local copies, waits for them, and re-layouts  0.69 us (2%)
    pallas_call x1, Pallas kernels, local(): pl.pallas_call(kernel, out_shape=jax.ShapeDtypeStruct((26, 16, 128), F32)...  36 us

profile of v7, /device:TPU:32, one launch (start us, length us, event | category | flops | bytes accessed | tf_op | source)
XLA Modules:
  0.0 36.7 jit_solution(13472977666269299912)
XLA Ops:
  0.0 36.0 %adjoint.1 = f32[26,16,128]{2,1,0:T(8,128)S(1)} custom-call(bf16[26,8,150]{2,1,0:T(8,128)(2,1)} %bitcast.10, bf16[2,150,16,1024]{3,2,1,0:T(8,128)(2,1)} %bitcast.9, f32[16]{0:T(128)} %prior_hbm.1, f32[1,1024]{1,0:T(1,128)} %bitcast.11), custom_call_target="tpu_custom_call" | custom-call | tf_op jit(solution)/shard_map/adjoint/pallas_call | solution.py:441
  36.0 0.7 %copy.7 = f32[26,2,1024]{2,1,0:T(2,128)} copy(f32[26,2,1024]{2,1,0:T(2,128)S(1)} %bitcast.8) | data formatting | bytes 425984
